TPU v7x, 128 devices: a whole 4x4x4 slice. The times are simulated.
128 devices in a mesh: vocab: 16 (over x, y), hid: 8 (over z, core).
Axes of the slice: x: 4, y: 4, z: 4, core: 2. Of those that a mesh axis runs over, the one named last changes fastest.
Arguments:
- hidden: bfloat16 [2, 512, 7168], P(None, 'vocab', 'hid'), may hold values from -100 to 100
- head_weight: bfloat16 [7168, 131072], P('hid', 'vocab'), may hold values from -2 to 2
- targets: int32 [2, 512], P(None, 'hid'), may hold values from 0 to 131071
Outputs:
- entropy: float32 [2, 512], P(None, 'hid')
- squared: float32 [2, 512], P(None, 'hid')
All inputs are finite; a program needn't handle non-finite values.
Results may differ from a plain program's by a relative error of at most 0.0003.
Values may be sent and summed in bfloat16 or wider, within the bound.
No kernel may reach another device: no remote copies, remote signals or barrier semaphores. Data moves between devices by JAX's collectives and lax.ppermute only.
A program may use at most 192 MiB of HBM per device.

v0:
```python
import jax
import jax.numpy as jnp
from jax import lax
from jax.experimental import pallas as pl
from jax.experimental.pallas import tpu as pltpu
from jax.sharding import Mesh
from jax.sharding import PartitionSpec as P

VOCAB = ("vocab_0", "vocab_1")
HID = ("hid_0", "hid_1")
EVERY = (*VOCAB, *HID)
RING = "hid_0"
CORE = "hid_1"
UP = [(i, (i + 1) % 4) for i in range(4)]
DOWN = [(i, (i - 1) % 4) for i in range(4)]
ACROSS = [(i, (i + 2) % 4) for i in range(4)]
SWAP = [(0, 1), (1, 0)]
WAYS = (UP, DOWN, ACROSS)
OFFSETS = (0, 3, 1, 2)
SCALE = 1.0 / 16.0


def packed(partial):
    return (partial * SCALE).astype(jnp.float16)


def unpacked(message):
    return message.astype(jnp.float32) * (1.0 / SCALE)


def dot(rows, columns):
    return jnp.dot(rows, columns, preferred_element_type=jnp.float32)


def after(value, *earlier):
    return lax.optimization_barrier((value, *earlier))[0]


def take(array, index, axis):
    return lax.dynamic_index_in_dim(array, index, axis, False)


def offset(k):
    return jnp.where(k == 0, 0, jnp.where(k == 1, 3, k - 1))


def fetch(given, kept, done):
    copy = pltpu.make_async_copy(given, kept, done)
    copy.start()
    copy.wait()


def resident(array):
    return pl.pallas_call(
        fetch,
        out_shape=pltpu.VMEM(array.shape, array.dtype),
        in_specs=[pl.BlockSpec(memory_space=pltpu.HBM)],
        out_specs=pl.BlockSpec(memory_space=pltpu.VMEM),
        scratch_shapes=[pltpu.SemaphoreType.DMA],
        compiler_params=pltpu.CompilerParams(vmem_limit_bytes=40 << 20),
        name="resident",
    )(array)


def losses(hidden, head_weight, targets):
    ring = lax.axis_index(RING)
    core = lax.axis_index(CORE)
    vocab_index = lax.axis_index(VOCAB)
    width = head_weight.shape[1]
    half = width // 2
    deal = hidden.shape[1] // 4
    weight = resident(head_weight)

    dealt = hidden.reshape(2, 4, deal, hidden.shape[2])
    dealt = jnp.stack([take(dealt, 1 - core, 0), take(dealt, core, 0)])
    dealt = jnp.stack([take(dealt, (ring + k) % 4, 1) for k in (2, 1, 3, 0)], axis=1)

    def token_of(row):
        plane_at = lax.rem(lax.axis_index(VOCAB[0]) + offset(row // (4 * deal)), 4)
        line_at = lax.rem(lax.axis_index(VOCAB[1]) + offset(row // deal % 4), 4)
        return 4 * deal * (4 * plane_at + line_at) + deal * ring + row % deal

    mine = lax.dynamic_slice_in_dim(targets, core, 1)
    mate = lax.dynamic_slice_in_dim(targets, 1 - core, 1)
    pair = jnp.concatenate([mine, lax.ppermute(mate, CORE, SWAP)])
    labels = 0
    for k, way in enumerate((None, *WAYS)):
        piece = pair if way is None else lax.ppermute(pair, RING, way)
        shape = (16 * deal, *piece.shape)
        side, place = (lax.broadcasted_iota(jnp.int32, shape, d) for d in (1, 2))
        owner = 2 * lax.rem(ring + OFFSETS[k], 4) + jnp.where(side == 0, core, 1 - core)
        wanted = token_of(lax.broadcasted_iota(jnp.int32, shape, 0))
        hit = owner * piece.shape[1] + place == wanted
        labels = labels + jnp.sum(jnp.where(hit, piece, 0), axis=(1, 2))

    def around(block, axis):
        return [lax.ppermute(block, axis, way) for way in WAYS]

    plane = [dealt, *around(dealt, VOCAB[1])]
    plane = jnp.stack(plane, axis=2).reshape(2, 4, 4 * deal, hidden.shape[2])
    far = around(plane[:, 0], VOCAB[0])
    rest = around(plane[:, 1:3], VOCAB[0])
    last = around(plane[:, 3], VOCAB[0])

    def given(rows, lo, size):
        partial = dot(rows[0], weight[:, lo : lo + size])
        return lax.ppermute(partial, CORE, SWAP)

    def both(rows, lo):
        found = given(rows, lo, half)
        return found + dot(rows[1], weight[:, lo : lo + half])

    far = jnp.concatenate([plane[:, 0], *far], axis=1)
    far_up = packed(both(far, 0))
    far_down = packed(both(far, half))
    rest = jnp.concatenate([plane[:, 1:3], *rest], axis=2)
    rest = after(rest, far_up, far_down)
    near_up = packed(both(rest[:, 0], half))
    near_down = packed(both(rest[:, 1], 0))
    rest = after(rest, near_up, near_down)
    sum_low = both(rest[:, 0], 0)
    sum_high = both(rest[:, 1], half)
    own = jnp.concatenate([plane[:, 3], *last], axis=1)
    own = after(own, sum_low, sum_high)
    far_up = lax.ppermute(far_up, RING, UP)
    far_down = lax.ppermute(far_down, RING, DOWN)
    near_up = lax.ppermute(near_up, RING, UP)
    near_down = lax.ppermute(near_down, RING, DOWN)
    sum_low, sum_high = lax.optimization_barrier((sum_low, sum_high))
    sum_up = lax.ppermute(packed(sum_low + unpacked(far_up)), RING, UP)
    sum_down = lax.ppermute(packed(sum_high + unpacked(far_down)), RING, DOWN)
    found = given(own, 0, width)
    both_halves = found + dot(own[1], weight)
    low, high = both_halves[:, :half], both_halves[:, half:]
    low, high = lax.optimization_barrier((low, high))
    low = low + unpacked(near_down)
    high = high + unpacked(near_up)
    low, high = lax.optimization_barrier((low, high))
    low = low + unpacked(sum_up)
    high = high + unpacked(sum_down)

    first = vocab_index * width
    ids = first + lax.broadcasted_iota(jnp.int32, low.shape, 1)
    peak = jnp.maximum(jnp.max(low, axis=1), jnp.max(high, axis=1))
    mass = jnp.sum(jnp.exp(low - peak[:, None]), axis=1) + jnp.sum(
        jnp.exp(high - peak[:, None]), axis=1
    )
    picked = jnp.sum(jnp.where(ids == labels[:, None], low, 0.0), axis=1) + jnp.sum(
        jnp.where(ids + half == labels[:, None], high, 0.0), axis=1
    )

    shape = (peak.shape[0], 8, 2 * deal)
    row, owner, place = (lax.broadcasted_iota(jnp.int32, shape, d) for d in range(3))
    token = targets.shape[1] * owner + 4 * deal * (place // deal) + place % deal
    hit = token + deal * ring == token_of(row)
    peak, mass, picked = (
        jnp.sum(jnp.where(hit, value[:, None, None], 0.0), axis=0)
        for value in (peak, mass, picked)
    )
    stats = jnp.concatenate([peak, mass, picked], axis=1)
    stats = stats.reshape(8, 1, -1)
    stats = jnp.broadcast_to(stats, (16, *stats.shape)).reshape(128, 1, -1)
    stats = lax.all_to_all(stats, EVERY, split_axis=0, concat_axis=0, tiled=True)
    stats = stats.reshape(16, 4, 2, -1)
    peaks, masses, picks = jnp.split(stats, 3, axis=-1)
    top = jnp.max(peaks, axis=0)
    total = jnp.sum(masses * jnp.exp(peaks - top), axis=0)
    log_norm = top + jnp.log(total)
    entropy = log_norm - jnp.sum(picks, axis=0)

    shape = (*entropy.shape, targets.shape[1])
    source, _, place, wanted = (lax.broadcasted_iota(jnp.int32, shape, d) for d in range(4))
    hit = 4 * deal * (place // deal) + deal * source + place % deal == wanted

    def in_order(values):
        return jnp.sum(jnp.where(hit, values[..., None], 0.0), axis=(0, 2))

    return in_order(entropy), in_order(log_norm * log_norm)


def solution(mesh):
    finer = Mesh(mesh.devices.reshape(4, 4, 4, 2), EVERY)
    return jax.shard_map(
        losses,
        mesh=finer,
        in_specs=(P(None, VOCAB, HID), P(HID, VOCAB), P(None, HID)),
        out_specs=(P(None, HID), P(None, HID)),
        check_vma=False,
    )
```

profile of v0, /device:TPU:1, one launch (start us, length us, event | category | flops | bytes accessed | tf_op | source)
XLA Modules:
  0.0 197.1 jit_solution(1350055573547684576)
XLA Ops:
  1.6 3.6 %collective-permute-start.1 = (bf16[2,4,8,896]{3,2,1,0:T(8,128)(2,1)S(1)}, bf16[2,4,8,896]{3,2,1,0:T(8,128)(2,1)S(1)}, u32[]{:S(2)}, u32[]{:S(2)}) collective-permute-start(bf16[2,4,8,896]{3,2,1,0:T(8,128)(2,1)S(1)} %get-tuple-element.43), channel_id=1, source_target_pairs={{0,24},{8,0},{16,8},{24,16},{1,25},{9,1},{17,9},{25,17},{2,26},{10... | collective-permute-start | bytes 344072 | tf_op jit(solution)/shard_map/ppermute | solution.py:97
  7.0 6.2 %collective-permute-done = bf16[2,4,8,896]{3,2,1,0:T(8,128)(2,1)S(1)} collective-permute-done((bf16[2,4,8,896]{3,2,1,0:T(8,128)(2,1)S(1)}, bf16[2,4,8,896]{3,2,1,0:T(8,128)(2,1)S(1)}, u32[]{:S(2)}, u32[]{:S(2)}) %collective-permute-start) | collective-permute-done | bytes 114720 | tf_op jit(solution)/shard_map/ppermute | solution.py:97
  13.4 2.8 %collective-permute-start.11 = (bf16[2,32,896]{2,1,0:T(8,128)(2,1)S(1)}, bf16[2,32,896]{2,1,0:T(8,128)(2,1)S(1)}, u32[]{:S(2)}, u32[]{:S(2)}) collective-permute-start(bf16[2,32,896]{2,1,0:T(8,128)(2,1)S(1)} %get-tuple-element.40), channel_id=1, source_target_pairs={{0,64},{32,96},{64,0},{96,32},{1,65},{33,97},{65,1},{97,33},{2,66}... | collective-permute-start | bytes 344072 | tf_op jit(solution)/shard_map/ppermute | solution.py:97
  17.7 5.2 %resident.1 = bf16[896,8192]{1,0:T(8,128)(2,1)S(1)} custom-call(bf16[896,8192]{1,0:T(8,128)(2,1)} %given.1), custom_call_target="tpu_custom_call" | custom-call | tf_op jit(solution)/shard_map/resident/pallas_call | solution.py:54
  30.7 5.5 %collective-permute-done.8 = bf16[2,2,32,896]{3,2,1,0:T(8,128)(2,1)S(1)} collective-permute-done((bf16[2,2,32,896]{3,2,1,0:T(8,128)(2,1)S(1)}, bf16[2,2,32,896]{3,2,1,0:T(8,128)(2,1)S(1)}, u32[]{:S(2)}, u32[]{:S(2)}) %collective-permute-start.8) | collective-permute-done | bytes 229408 | tf_op jit(solution)/shard_map/ppermute | solution.py:97
  36.1 4.6 %collective-permute-done.7 = bf16[2,2,32,896]{3,2,1,0:T(8,128)(2,1)S(1)} collective-permute-done((bf16[2,2,32,896]{3,2,1,0:T(8,128)(2,1)S(1)}, bf16[2,2,32,896]{3,2,1,0:T(8,128)(2,1)S(1)}, u32[]{:S(2)}, u32[]{:S(2)}) %collective-permute-start.7) | collective-permute-done | bytes 229408 | tf_op jit(solution)/shard_map/ppermute | solution.py:97
  42.0 2.4 %fusion.4 = f16[128,4096]{1,0:T(8,128)(2,1)} fusion(f32[128,4096]{1,0:T(8,128)S(1)} %collective-permute-done.12, bf16[896,8192]{1,0:T(8,128)(2,1)S(1)} %resident.1, bf16[2,128,896]{2,1,0:T(8,128)(2,1)S(1)} %pad_maximum_fusion.2), kind=kOutput, calls=%fused_computation.11 | convolution fusion | flops 941096960 | bytes 10715136 | tf_op jit(solution)/shard_map/dot_general | solution.py:32
  44.3 2.4 %fusion.5 = f16[128,4096]{1,0:T(8,128)(2,1)} fusion(f32[128,4096]{1,0:T(8,128)S(1)} %collective-permute-done.13, bf16[896,8192]{1,0:T(8,128)(2,1)S(1)} %resident.1, bf16[2,128,896]{2,1,0:T(8,128)(2,1)S(1)} %pad_maximum_fusion.2), kind=kOutput, calls=%fused_computation.12 | convolution fusion | flops 941096960 | bytes 10715136 | tf_op jit(solution)/shard_map/dot_general | solution.py:32
  50.1 2.2 %collective-permute-done.14 = f32[128,4096]{1,0:T(8,128)S(1)} collective-permute-done((f32[128,4096]{1,0:T(8,128)S(1)}, f32[128,4096]{1,0:T(8,128)S(1)}, u32[]{:S(2)}, u32[]{:S(2)}) %collective-permute-start.14) | collective-permute-done | bytes 2097184 | tf_op jit(solution)/shard_map/ppermute | solution.py:107
  52.3 2.4 %fusion.6 = f16[128,4096]{1,0:T(8,128)(2,1)} fusion(f32[128,4096]{1,0:T(8,128)S(1)} %collective-permute-done.14, bf16[896,8192]{1,0:T(8,128)(2,1)S(1)} %resident.1, bf16[2,2,128,896]{3,2,1,0:T(8,128)(2,1)S(1)} %pad_maximum_fusion), kind=kOutput, calls=%fused_computation.13 | convolution fusion | flops 941096960 | bytes 10715136 | tf_op jit(solution)/shard_map/dot_general | solution.py:32
  55.3 2.3 %fusion.7 = f16[128,4096]{1,0:T(8,128)(2,1)} fusion(f32[128,4096]{1,0:T(8,128)S(1)} %collective-permute-done.15, bf16[896,8192]{1,0:T(8,128)(2,1)S(1)} %resident.1, bf16[2,2,128,896]{3,2,1,0:T(8,128)(2,1)S(1)} %pad_maximum_fusion), kind=kOutput, calls=%fused_computation.14 | convolution fusion | flops 941096960 | bytes 10715136 | tf_op jit(solution)/shard_map/dot_general | solution.py:32
  63.5 3.1 %collective-permute-done.5 = bf16[2,32,896]{2,1,0:T(8,128)(2,1)S(1)} collective-permute-done((bf16[2,32,896]{2,1,0:T(8,128)(2,1)S(1)}, bf16[2,32,896]{2,1,0:T(8,128)(2,1)S(1)}, u32[]{:S(2)}, u32[]{:S(2)}) %collective-permute-start.5) | collective-permute-done | bytes 114720 | tf_op jit(solution)/shard_map/ppermute | solution.py:97
  70.7 2.6 %convolution_add_fusion.1 = f32[128,4096]{1,0:T(8,128)} fusion(f32[128,4096]{1,0:T(8,128)S(1)} %collective-permute-done.17, bf16[896,8192]{1,0:T(8,128)(2,1)S(1)} %resident.1, bf16[2,2,128,896]{3,2,1,0:T(8,128)(2,1)S(1)} %pad_maximum_fusion), kind=kOutput, calls=%fused_computation.1 | convolution fusion | flops 940048384 | bytes 11763712 | tf_op jit(solution)/shard_map/dot_general | solution.py:32
  73.3 4.4 %fusion.29 = f32[128,8192]{1,0:T(8,128)} fusion(bf16[896,8192]{1,0:T(8,128)(2,1)S(1)} %resident.1, bf16[2,128,896]{2,1,0:T(8,128)(2,1)S(1)} %pad_maximum_fusion.1), kind=kOutput, calls=%fused_computation.52 | convolution fusion | flops 1879048192 | bytes 19103744 | tf_op jit(solution)/shard_map/dot_general | solution.py:32
  79.3 4.0 %collective-permute-start.23 = (f16[128,4096]{1,0:T(8,128)(2,1)}, f16[128,4096]{1,0:T(8,128)(2,1)}, u32[]{:S(2)}, u32[]{:S(2)}) collective-permute-start(f16[128,4096]{1,0:T(8,128)(2,1)} %fusion.5), channel_id=1, source_target_pairs={{0,6},{2,0},{4,2},{6,4},{1,7},{3,1},{5,3},{7,5},{8,14},{10,8},{12,... | collective-permute-start | bytes 3145736 | tf_op jit(solution)/shard_map/ppermute | solution.py:126
  83.3 2.8 %collective-permute-done.25 = s32[1,64]{1,0:T(1,128)S(1)} collective-permute-done((s32[1,64]{1,0:T(1,128)S(1)}, s32[1,64]{1,0:T(1,128)S(1)}, u32[]{:S(2)}, u32[]{:S(2)}) %collective-permute-start.25) | collective-permute-done | bytes 288 | tf_op jit(solution)/shard_map/ppermute | solution.py:85
  86.2 3.6 %collective-permute-start.28 = (s32[2,64]{1,0:T(2,128)S(1)}, s32[2,64]{1,0:T(2,128)S(1)}, u32[]{:S(2)}, u32[]{:S(2)}) collective-permute-start(s32[2,64]{1,0:T(2,128)S(1)} %pad_add_fusion), channel_id=1, source_target_pairs={{0,4},{2,6},{4,0},{6,2},{1,5},{3,7},{5,1},{7,3},{8,12},{10,14},{12... | collective-permute-start | bytes 1544 | tf_op jit(solution)/shard_map/ppermute | solution.py:88
  91.4 14.3 %collective-permute-done.27 = s32[2,64]{1,0:T(2,128)S(1)} collective-permute-done((s32[2,64]{1,0:T(2,128)S(1)}, s32[2,64]{1,0:T(2,128)S(1)}, u32[]{:S(2)}, u32[]{:S(2)}) %collective-permute-start.27) | collective-permute-done | bytes 544 | tf_op jit(solution)/shard_map/ppermute | solution.py:88
  113.2 18.6 %collective-permute-done.21 = f16[128,4096]{1,0:T(8,128)(2,1)S(1)} collective-permute-done((f16[128,4096]{1,0:T(8,128)(2,1)}, f16[128,4096]{1,0:T(8,128)(2,1)S(1)}, u32[]{:S(2)}, u32[]{:S(2)}) %collective-permute-start.21) | collective-permute-done | bytes 1048608 | tf_op jit(solution)/shard_map/ppermute | solution.py:125
  132.3 8.7 %convolution_add_fusion = f32[128,8192]{1,0:T(8,128)S(1)} fusion(f32[128,8192]{1,0:T(8,128)} %collective-permute-done.18, bf16[896,8192]{1,0:T(8,128)(2,1)} %copy-done, bf16[2,128,896]{2,1,0:T(8,128)(2,1)S(1)} %pad_maximum_fusion.1), kind=kOutput, calls=%fused_computation | convolution fusion | flops 1880096768 | bytes 23298048 | tf_op jit(solution)/shard_map/dot_general | solution.py:32
  141.7 12.6 %collective-permute-done.20 = f16[128,4096]{1,0:T(8,128)(2,1)S(1)} collective-permute-done((f16[128,4096]{1,0:T(8,128)(2,1)}, f16[128,4096]{1,0:T(8,128)(2,1)S(1)}, u32[]{:S(2)}, u32[]{:S(2)}) %collective-permute-start.20) | collective-permute-done | bytes 1048608 | tf_op jit(solution)/shard_map/ppermute | solution.py:127
  154.6 22.1 %collective-permute-done.22 = f16[128,4096]{1,0:T(8,128)(2,1)S(1)} collective-permute-done((f16[128,4096]{1,0:T(8,128)(2,1)S(1)}, f16[128,4096]{1,0:T(8,128)(2,1)S(1)}, u32[]{:S(2)}, u32[]{:S(2)}) %collective-permute-start.22) | collective-permute-done | bytes 1048608 | tf_op jit(solution)/shard_map/ppermute | solution.py:130
  180.2 6.6 %all-to-all-start = ((f32[128,1,48]{2,1,0:T(1,128)}), f32[128,1,48]{2,1,0:T(1,128)S(1)}, u32[]{:S(2)}, u32[]{:S(2)}) async-start(f32[128,1,48]{2,1,0:T(1,128)} %bitcast.23), calls=%async_computation | async-start | bytes 131072 | tf_op jit(solution)/shard_map/all_to_all | solution.py:163
  186.8 9.4 %all-to-all-done = f32[128,1,48]{2,1,0:T(1,128)S(1)} async-done(((f32[128,1,48]{2,1,0:T(1,128)}), f32[128,1,48]{2,1,0:T(1,128)S(1)}, u32[]{:S(2)}, u32[]{:S(2)}) %all-to-all-start) | async-done | bytes 24608 | tf_op jit(solution)/shard_map/all_to_all | solution.py:163
  (100 shorter events, 43.6 us)
Async XLA Ops:
  5.3 8.0 %collective-permute-start = (bf16[2,4,8,896]{3,2,1,0:T(8,128)(2,1)S(1)}, bf16[2,4,8,896]{3,2,1,0:T(8,128)(2,1)S(1)}, u32[]{:S(2)}, u32[]{:S(2)}) collective-permute-start(bf16[2,4,8,896]{3,2,1,0:T(8,128)(2,1)S(1)} %get-tuple-element.43), channel_id=1, source_target_pairs={{0,8},{8,16},{16,24},{24,0},{1,9},{9,17},{17,25},{25,1},{2,10},{10... | collective-permute-start | bytes 344072 | tf_op jit(solution)/shard_map/ppermute | solution.py:97
  5.3 8.0 %collective-permute-start.2 = (bf16[2,4,8,896]{3,2,1,0:T(8,128)(2,1)S(1)}, bf16[2,4,8,896]{3,2,1,0:T(8,128)(2,1)S(1)}, u32[]{:S(2)}, u32[]{:S(2)}) collective-permute-start(bf16[2,4,8,896]{3,2,1,0:T(8,128)(2,1)S(1)} %get-tuple-element.43), channel_id=1, source_target_pairs={{0,16},{8,24},{16,0},{24,8},{1,17},{9,25},{17,1},{25,9},{2,18},{10... | collective-permute-start | bytes 344072 | tf_op jit(solution)/shard_map/ppermute | solution.py:97
  13.4 9.5 %collective-permute-start.11 = (bf16[2,32,896]{2,1,0:T(8,128)(2,1)S(1)}, bf16[2,32,896]{2,1,0:T(8,128)(2,1)S(1)}, u32[]{:S(2)}, u32[]{:S(2)}) collective-permute-start(bf16[2,32,896]{2,1,0:T(8,128)(2,1)S(1)} %get-tuple-element.40), channel_id=1, source_target_pairs={{0,64},{32,96},{64,0},{96,32},{1,65},{33,97},{65,1},{97,33},{2,66}... | collective-permute-start | bytes 344072 | tf_op jit(solution)/shard_map/ppermute | solution.py:97
  16.2 6.7 %collective-permute-start.10 = (bf16[2,32,896]{2,1,0:T(8,128)(2,1)S(1)}, bf16[2,32,896]{2,1,0:T(8,128)(2,1)S(1)}, u32[]{:S(2)}, u32[]{:S(2)}) collective-permute-start(bf16[2,32,896]{2,1,0:T(8,128)(2,1)S(1)} %get-tuple-element.40), channel_id=1, source_target_pairs={{0,96},{32,0},{64,32},{96,64},{1,97},{33,1},{65,33},{97,65},{2,98}... | collective-permute-start | bytes 344072 | tf_op jit(solution)/shard_map/ppermute | solution.py:97
  24.3 17.7 %collective-permute-start.12 = (f32[128,4096]{1,0:T(8,128)S(1)}, f32[128,4096]{1,0:T(8,128)S(1)}, u32[]{:S(2)}, u32[]{:S(2)}) collective-permute-start(f32[128,4096]{1,0:T(8,128)S(1)} %fusion.24), channel_id=1, source_target_pairs={{0,1},{1,0},{2,3},{3,2},{4,5},{5,4},{6,7},{7,6},{8,9},{9,8},{10,11... | collective-permute-start | bytes 6291464 | tf_op jit(solution)/shard_map/ppermute | solution.py:107
  27.7 16.6 %collective-permute-start.13 = (f32[128,4096]{1,0:T(8,128)S(1)}, f32[128,4096]{1,0:T(8,128)S(1)}, u32[]{:S(2)}, u32[]{:S(2)}) collective-permute-start(f32[128,4096]{1,0:T(8,128)S(1)} %fusion.15), channel_id=1, source_target_pairs={{0,1},{1,0},{2,3},{3,2},{4,5},{5,4},{6,7},{7,6},{8,9},{9,8},{10,11... | collective-permute-start | bytes 6291464 | tf_op jit(solution)/shard_map/ppermute | solution.py:107
  27.9 8.3 %collective-permute-start.8 = (bf16[2,2,32,896]{3,2,1,0:T(8,128)(2,1)S(1)}, bf16[2,2,32,896]{3,2,1,0:T(8,128)(2,1)S(1)}, u32[]{:S(2)}, u32[]{:S(2)}) collective-permute-start(bf16[2,2,32,896]{3,2,1,0:T(8,128)(2,1)S(1)} %slice.112), channel_id=1, source_target_pairs={{0,64},{32,96},{64,0},{96,32},{1,65},{33,97},{65,1},{97,33},{2,66}... | collective-permute-start | bytes 688136 | tf_op jit(solution)/shard_map/ppermute | solution.py:97
  28.7 12.0 %collective-permute-start.7 = (bf16[2,2,32,896]{3,2,1,0:T(8,128)(2,1)S(1)}, bf16[2,2,32,896]{3,2,1,0:T(8,128)(2,1)S(1)}, u32[]{:S(2)}, u32[]{:S(2)}) collective-permute-start(bf16[2,2,32,896]{3,2,1,0:T(8,128)(2,1)S(1)} %slice.112), channel_id=1, source_target_pairs={{0,96},{32,0},{64,32},{96,64},{1,97},{33,1},{65,33},{97,65},{2,98}... | collective-permute-start | bytes 688136 | tf_op jit(solution)/shard_map/ppermute | solution.py:97
  30.7 11.2 %collective-permute-start.6 = (bf16[2,2,32,896]{3,2,1,0:T(8,128)(2,1)S(1)}, bf16[2,2,32,896]{3,2,1,0:T(8,128)(2,1)S(1)}, u32[]{:S(2)}, u32[]{:S(2)}) collective-permute-start(bf16[2,2,32,896]{3,2,1,0:T(8,128)(2,1)S(1)} %slice.112), channel_id=1, source_target_pairs={{0,32},{32,64},{64,96},{96,0},{1,33},{33,65},{65,97},{97,1},{2,34}... | collective-permute-start | bytes 688136 | tf_op jit(solution)/shard_map/ppermute | solution.py:97
  58.9 10.5 %collective-permute-start.16 = (f32[128,4096]{1,0:T(8,128)S(1)}, f32[128,4096]{1,0:T(8,128)S(1)}, u32[]{:S(2)}, u32[]{:S(2)}) collective-permute-start(f32[128,4096]{1,0:T(8,128)S(1)} %fusion.18), channel_id=1, source_target_pairs={{0,1},{1,0},{2,3},{3,2},{4,5},{5,4},{6,7},{7,6},{8,9},{9,8},{10,11... | collective-permute-start | bytes 6291464 | tf_op jit(solution)/shard_map/ppermute | solution.py:107
  60.6 10.1 %collective-permute-start.17 = (f32[128,4096]{1,0:T(8,128)S(1)}, f32[128,4096]{1,0:T(8,128)S(1)}, u32[]{:S(2)}, u32[]{:S(2)}) collective-permute-start(f32[128,4096]{1,0:T(8,128)S(1)} %fusion.9), channel_id=1, source_target_pairs={{0,1},{1,0},{2,3},{3,2},{4,5},{5,4},{6,7},{7,6},{8,9},{9,8},{10,11... | collective-permute-start | bytes 6291464 | tf_op jit(solution)/shard_map/ppermute | solution.py:107
  60.8 5.8 %collective-permute-start.5 = (bf16[2,32,896]{2,1,0:T(8,128)(2,1)S(1)}, bf16[2,32,896]{2,1,0:T(8,128)(2,1)S(1)}, u32[]{:S(2)}, u32[]{:S(2)}) collective-permute-start(bf16[2,32,896]{2,1,0:T(8,128)(2,1)S(1)} %get-tuple-element.41), channel_id=1, source_target_pairs={{0,64},{32,96},{64,0},{96,32},{1,65},{33,97},{65,1},{97,33},{2,66}... | collective-permute-start | bytes 344072 | tf_op jit(solution)/shard_map/ppermute | solution.py:97
  61.8 7.0 %collective-permute-start.4 = (bf16[2,32,896]{2,1,0:T(8,128)(2,1)S(1)}, bf16[2,32,896]{2,1,0:T(8,128)(2,1)S(1)}, u32[]{:S(2)}, u32[]{:S(2)}) collective-permute-start(bf16[2,32,896]{2,1,0:T(8,128)(2,1)S(1)} %get-tuple-element.41), channel_id=1, source_target_pairs={{0,96},{32,0},{64,32},{96,64},{1,97},{33,1},{65,33},{97,65},{2,98}... | collective-permute-start | bytes 344072 | tf_op jit(solution)/shard_map/ppermute | solution.py:97
  77.7 54.6 %collective-permute-start.18 = (f32[128,8192]{1,0:T(8,128)}, f32[128,8192]{1,0:T(8,128)}, u32[]{:S(2)}, u32[]{:S(2)}) collective-permute-start(f32[128,8192]{1,0:T(8,128)} %fusion.29), channel_id=1, source_target_pairs={{0,1},{1,0},{2,3},{3,2},{4,5},{5,4},{6,7},{7,6},{8,9},{9,8},{10,11... | collective-permute-start | bytes 12582920 | tf_op jit(solution)/shard_map/ppermute | solution.py:107
  79.1 7.1 %collective-permute-start.25 = (s32[1,64]{1,0:T(1,128)S(1)}, s32[1,64]{1,0:T(1,128)S(1)}, u32[]{:S(2)}, u32[]{:S(2)}) collective-permute-start(s32[1,64]{1,0:T(1,128)S(1)} %get-tuple-element.53), channel_id=1, source_target_pairs={{0,1},{1,0},{2,3},{3,2},{4,5},{5,4},{6,7},{7,6},{8,9},{9,8},{10,11... | collective-permute-start | bytes 776 | tf_op jit(solution)/shard_map/ppermute | solution.py:85
  79.3 30.5 %collective-permute-start.23 = (f16[128,4096]{1,0:T(8,128)(2,1)}, f16[128,4096]{1,0:T(8,128)(2,1)}, u32[]{:S(2)}, u32[]{:S(2)}) collective-permute-start(f16[128,4096]{1,0:T(8,128)(2,1)} %fusion.5), channel_id=1, source_target_pairs={{0,6},{2,0},{4,2},{6,4},{1,7},{3,1},{5,3},{7,5},{8,14},{10,8},{12,... | collective-permute-start | bytes 3145736 | tf_op jit(solution)/shard_map/ppermute | solution.py:126
  89.8 15.9 %collective-permute-start.27 = (s32[2,64]{1,0:T(2,128)S(1)}, s32[2,64]{1,0:T(2,128)S(1)}, u32[]{:S(2)}, u32[]{:S(2)}) collective-permute-start(s32[2,64]{1,0:T(2,128)S(1)} %pad_add_fusion), channel_id=1, source_target_pairs={{0,6},{2,0},{4,2},{6,4},{1,7},{3,1},{5,3},{7,5},{8,14},{10,8},{12,... | collective-permute-start | bytes 1544 | tf_op jit(solution)/shard_map/ppermute | solution.py:88
  90.2 15.5 %collective-permute-start.26 = (s32[2,64]{1,0:T(2,128)S(1)}, s32[2,64]{1,0:T(2,128)S(1)}, u32[]{:S(2)}, u32[]{:S(2)}) collective-permute-start(s32[2,64]{1,0:T(2,128)S(1)} %pad_add_fusion), channel_id=1, source_target_pairs={{0,2},{2,4},{4,6},{6,0},{1,3},{3,5},{5,7},{7,1},{8,10},{10,12},{12... | collective-permute-start | bytes 1544 | tf_op jit(solution)/shard_map/ppermute | solution.py:88
  105.9 25.9 %collective-permute-start.21 = (f16[128,4096]{1,0:T(8,128)(2,1)}, f16[128,4096]{1,0:T(8,128)(2,1)S(1)}, u32[]{:S(2)}, u32[]{:S(2)}) collective-permute-start(f16[128,4096]{1,0:T(8,128)(2,1)} %fusion.4), channel_id=1, source_target_pairs={{0,2},{2,4},{4,6},{6,0},{1,3},{3,5},{5,7},{7,1},{8,10},{10,12},{12... | collective-permute-start | bytes 3145736 | tf_op jit(solution)/shard_map/ppermute | solution.py:125
  107.1 47.2 %collective-permute-start.20 = (f16[128,4096]{1,0:T(8,128)(2,1)}, f16[128,4096]{1,0:T(8,128)(2,1)S(1)}, u32[]{:S(2)}, u32[]{:S(2)}) collective-permute-start(f16[128,4096]{1,0:T(8,128)(2,1)} %fusion.6), channel_id=1, source_target_pairs={{0,2},{2,4},{4,6},{6,0},{1,3},{3,5},{5,7},{7,1},{8,10},{10,12},{12... | collective-permute-start | bytes 3145736 | tf_op jit(solution)/shard_map/ppermute | solution.py:127
  107.7 33.6 %collective-permute-start.19 = (f16[128,4096]{1,0:T(8,128)(2,1)}, f16[128,4096]{1,0:T(8,128)(2,1)S(1)}, u32[]{:S(2)}, u32[]{:S(2)}) collective-permute-start(f16[128,4096]{1,0:T(8,128)(2,1)} %fusion.7), channel_id=1, source_target_pairs={{0,6},{2,0},{4,2},{6,4},{1,7},{3,1},{5,3},{7,5},{8,14},{10,8},{12,... | collective-permute-start | bytes 3145736 | tf_op jit(solution)/shard_map/ppermute | solution.py:128
  112.0 65.1 %collective-permute-start.24 = (f16[128,4096]{1,0:T(8,128)(2,1)S(1)}, f16[128,4096]{1,0:T(8,128)(2,1)S(1)}, u32[]{:S(2)}, u32[]{:S(2)}) collective-permute-start(f16[128,4096]{1,0:T(8,128)(2,1)S(1)} %multiply_convert_fusion), channel_id=1, source_target_pairs={{0,6},{2,0},{4,2},{6,4},{1,7},{3,1},{5,3},{7,5},{8,14},{10,8},{12,... | collective-permute-start | bytes 3145736 | tf_op jit(solution)/shard_map/ppermute | solution.py:131
  132.2 44.6 %collective-permute-start.22 = (f16[128,4096]{1,0:T(8,128)(2,1)S(1)}, f16[128,4096]{1,0:T(8,128)(2,1)S(1)}, u32[]{:S(2)}, u32[]{:S(2)}) collective-permute-start(f16[128,4096]{1,0:T(8,128)(2,1)S(1)} %multiply_convert_fusion.1), channel_id=1, source_target_pairs={{0,2},{2,4},{4,6},{6,0},{1,3},{3,5},{5,7},{7,1},{8,10},{10,12},{12... | collective-permute-start | bytes 3145736 | tf_op jit(solution)/shard_map/ppermute | solution.py:130
  180.2 16.0 %all-to-all-start = ((f32[128,1,48]{2,1,0:T(1,128)}), f32[128,1,48]{2,1,0:T(1,128)S(1)}, u32[]{:S(2)}, u32[]{:S(2)}) async-start(f32[128,1,48]{2,1,0:T(1,128)} %bitcast.23), calls=%async_computation | async-start | bytes 131072 | tf_op jit(solution)/shard_map/all_to_all | solution.py:163
  (8 other events, 88.2 us)
where the time goes:
time: 197 us
  waiting for transfers between devices  106 us (54%)
  starting transfers between devices  41.2 us (21%)
  matrix products  34 us (17%)
  other arithmetic  7.64 us (4%)
  Pallas kernels  5.18 us (3%)
    dot_general x14, matrix products, dot(): return jnp.dot(rows, columns, preferred_element_type=jnp.float32)  34 us
    ppermute x12, waiting for transfers between devices, around(): return [lax.ppermute(block, axis, way) for way in WAYS]  23.4 us
    ppermute x1, waiting for transfers between devices, losses(): sum_up = lax.ppermute(packed(sum_low + unpacked(far_up)), RING, UP)  22.1 us
    ppermute x1, waiting for transfers between devices, losses(): far_up = lax.ppermute(far_up, RING, UP)  18.6 us
    ppermute x12, starting transfers between devices, around(): return [lax.ppermute(block, axis, way) for way in WAYS]  15.1 us
    ppermute x3, waiting for transfers between devices, losses(): piece = pair if way is None else lax.ppermute(pair, RING, way)  14.3 us
    ppermute x1, waiting for transfers between devices, losses(): near_up = lax.ppermute(near_up, RING, UP)  12.6 us
    all_to_all x1, waiting for transfers between devices, losses(): lax.all_to_all(stats, EVERY, split_axis=0, concat_axis=0, tiled=True)  9.35 us
  transfers between devices with their start and end apart: 30, of which 16 were waited for; matrix products, arithmetic and copies ran while one was open for 12% of the time, Pallas kernels for 3%

commit v1 on v0

--- a/solution.py
+++ b/solution.py
@@ -15,6 +15,8 @@
 DOWN = [(i, (i - 1) % 4) for i in range(4)]
 ACROSS = [(i, (i + 2) % 4) for i in range(4)]
 SWAP = [(0, 1), (1, 0)]
+BESIDE = [(i, i ^ 1) for i in range(4)]
+BETWEEN = [(i, 3 - i) for i in range(4)]
 WAYS = (UP, DOWN, ACROSS)
 OFFSETS = (0, 3, 1, 2)
 SCALE = 1.0 / 16.0
@@ -42,6 +44,11 @@
 
 def offset(k):
     return jnp.where(k == 0, 0, jnp.where(k == 1, 3, k - 1))
+
+
+def met(here, k):
+    beside = lax.bitwise_xor(here, 1)
+    return jnp.where(k == 0, here, jnp.where(k == 1, beside, jnp.where(k == 2, 3 - here, 3 - beside)))
 
 
 def fetch(given, kept, done):
@@ -67,7 +74,7 @@
     core = lax.axis_index(CORE)
     vocab_index = lax.axis_index(VOCAB)
     width = head_weight.shape[1]
-    half = width // 2
+    half = width // 2 + 128
     deal = hidden.shape[1] // 4
     weight = resident(head_weight)
 
@@ -76,7 +83,7 @@
     dealt = jnp.stack([take(dealt, (ring + k) % 4, 1) for k in (2, 1, 3, 0)], axis=1)
 
     def token_of(row):
-        plane_at = lax.rem(lax.axis_index(VOCAB[0]) + offset(row // (4 * deal)), 4)
+        plane_at = met(lax.axis_index(VOCAB[0]), row // (4 * deal))
         line_at = lax.rem(lax.axis_index(VOCAB[1]) + offset(row // deal % 4), 4)
         return 4 * deal * (4 * plane_at + line_at) + deal * ring + row % deal
 
@@ -98,29 +105,40 @@
 
     plane = [dealt, *around(dealt, VOCAB[1])]
     plane = jnp.stack(plane, axis=2).reshape(2, 4, 4 * deal, hidden.shape[2])
-    far = around(plane[:, 0], VOCAB[0])
-    rest = around(plane[:, 1:3], VOCAB[0])
-    last = around(plane[:, 3], VOCAB[0])
+    back, ahead, away = around(plane[:, 0], VOCAB[0])
+    even = lax.axis_index(VOCAB[0]) % 2 == 0
+    beside, between = jnp.where(even, ahead, back), jnp.where(even, back, ahead)
+    far = jnp.concatenate([plane[:, 0], beside, between, away], axis=1)
+
+    one, three = plane[:, 1], plane[:, 2]
+    one = jnp.concatenate([one, lax.ppermute(one, VOCAB[0], BESIDE)], axis=1)
+    three = jnp.concatenate([three, lax.ppermute(three, VOCAB[0], BETWEEN)], axis=1)
+    more_one = lax.ppermute(one, VOCAB[0], BETWEEN)
+    more_three = lax.ppermute(three, VOCAB[0], BESIDE)
+    own = plane[:, 3]
+    own = jnp.concatenate([own, lax.ppermute(own, VOCAB[0], BESIDE)], axis=1)
+    own = jnp.concatenate([own, lax.ppermute(own, VOCAB[0], BETWEEN)], axis=1)
 
     def given(rows, lo, size):
-        partial = dot(rows[0], weight[:, lo : lo + size])
-        return lax.ppermute(partial, CORE, SWAP)
+        partial = packed(dot(rows[0], weight[:, lo : lo + size]))
+        return unpacked(lax.ppermute(partial, CORE, SWAP))
 
     def both(rows, lo):
-        found = given(rows, lo, half)
-        return found + dot(rows[1], weight[:, lo : lo + half])
-
-    far = jnp.concatenate([plane[:, 0], *far], axis=1)
+        size = half if lo == 0 else width - half
+        found = given(rows, lo, size)
+        return found + dot(rows[1], weight[:, lo : lo + size])
+
     far_up = packed(both(far, 0))
     far_down = packed(both(far, half))
-    rest = jnp.concatenate([plane[:, 1:3], *rest], axis=2)
-    rest = after(rest, far_up, far_down)
-    near_up = packed(both(rest[:, 0], half))
-    near_down = packed(both(rest[:, 1], 0))
-    rest = after(rest, near_up, near_down)
-    sum_low = both(rest[:, 0], 0)
-    sum_high = both(rest[:, 1], half)
-    own = jnp.concatenate([plane[:, 3], *last], axis=1)
+    one = jnp.concatenate([one, more_one], axis=1)
+    each = jnp.split(three, 2, axis=1), jnp.split(more_three, 2, axis=1)
+    three = jnp.concatenate([each[0][0], each[1][0], each[0][1], each[1][1]], axis=1)
+    one, three, *_ = lax.optimization_barrier((one, three, far_up, far_down))
+    near_up = packed(both(one, half))
+    near_down = packed(both(three, 0))
+    one, three, *_ = lax.optimization_barrier((one, three, near_up, near_down))
+    sum_low = both(one, 0)
+    sum_high = both(three, half)
     own = after(own, sum_low, sum_high)
     far_up = lax.ppermute(far_up, RING, UP)
     far_down = lax.ppermute(far_down, RING, DOWN)
@@ -139,15 +157,18 @@
     low = low + unpacked(sum_up)
     high = high + unpacked(sum_down)
 
+    def statistics(logits, first):
+        ids = first + lax.broadcasted_iota(jnp.int32, logits.shape, 1)
+        peak = jnp.max(logits, axis=1)
+        mass = jnp.sum(jnp.exp(logits - peak[:, None]), axis=1)
+        return peak, mass, jnp.sum(jnp.where(ids == labels[:, None], logits, 0.0), axis=1)
+
     first = vocab_index * width
-    ids = first + lax.broadcasted_iota(jnp.int32, low.shape, 1)
-    peak = jnp.maximum(jnp.max(low, axis=1), jnp.max(high, axis=1))
-    mass = jnp.sum(jnp.exp(low - peak[:, None]), axis=1) + jnp.sum(
-        jnp.exp(high - peak[:, None]), axis=1
-    )
-    picked = jnp.sum(jnp.where(ids == labels[:, None], low, 0.0), axis=1) + jnp.sum(
-        jnp.where(ids + half == labels[:, None], high, 0.0), axis=1
-    )
+    low_peak, low_mass, low_picked = statistics(low, first)
+    high_peak, high_mass, high_picked = statistics(high, first + half)
+    peak = jnp.maximum(low_peak, high_peak)
+    mass = low_mass * jnp.exp(low_peak - peak) + high_mass * jnp.exp(high_peak - peak)
+    picked = low_picked + high_picked
 
     shape = (peak.shape[0], 8, 2 * deal)
     row, owner, place = (lax.broadcasted_iota(jnp.int32, shape, d) for d in range(3))

time: 197 us -> 169 us (0.86)
  waiting for transfers between devices: 106 us -> 75.8 us
  local copies, waits for them, and re-layouts: 1.82 us -> 4.29 us
  other arithmetic: 7.64 us -> 5.6 us
  starting transfers between devices: 41.2 us -> 43.2 us
    ppermute x12 -> x6, waiting for transfers between devices: 23.4 us -> 3.99 us  [around(): return [lax.ppermute(block, axis, way) for way in WAYS]]
    ppermute x1, waiting for transfers between devices: 18.6 us -> 0.48 us  [losses(): far_up = lax.ppermute(far_up, RING, UP)]
    ppermute x1, waiting for transfers between devices: 0.01 us -> 15.2 us  [losses(): near_down = lax.ppermute(near_down, RING, DOWN)]
    ppermute x3, waiting for transfers between devices: 14.3 us -> 0.01 us  [losses(): piece = pair if way is None else lax.ppermute(pair, RING, way)]
    ppermute x1, waiting for transfers between devices: 0.01 us -> 12.8 us  [losses(): far_down = lax.ppermute(far_down, RING, DOWN)]
    ppermute x1, waiting for transfers between devices: 12.6 us -> 1.29 us  [losses(): near_up = lax.ppermute(near_up, RING, UP)]
    ppermute x7 -> x13, starting transfers between devices: 5.1 us -> 15.8 us  [the longest x7 8.83 us: given(): return unpacked(lax.ppermute(partial, CORE, SWAP))]
    ppermute x7 -> x13, waiting for transfers between devices: 2.89 us -> 9.71 us  [the longest x1 5.51 us: losses(): one = jnp.concatenate([one, lax.ppermute(one, VOCAB[0], BESIDE)], axis=1)]
  transfers between devices with their start and end apart: 30 -> 30, of which waited for: 16 -> 10; matrix products, arithmetic and copies ran while one was open for 12% -> 22% of each run, Pallas kernels for 3% -> 3%
where the time goes in v1:
time: 169 us
  waiting for transfers between devices  75.8 us (45%)
  starting transfers between devices  43.2 us (26%)
  matrix products  33.5 us (20%)
  other arithmetic  5.6 us (3%)
  Pallas kernels  5.18 us (3%)
  local copies, waits for them, and re-layouts  4.29 us (3%)
    dot_general x14, matrix products, dot(): return jnp.dot(rows, columns, preferred_element_type=jnp.float32)  33.5 us
    ppermute x1, waiting for transfers between devices, losses(): sum_up = lax.ppermute(packed(sum_low + unpacked(far_up)), RING, UP)  22.9 us
    ppermute x1, waiting for transfers between devices, losses(): near_down = lax.ppermute(near_down, RING, DOWN)  15.2 us
    ppermute x1, waiting for transfers between devices, losses(): far_down = lax.ppermute(far_down, RING, DOWN)  12.8 us
    all_to_all x1, waiting for transfers between devices, losses(): lax.all_to_all(stats, EVERY, split_axis=0, concat_axis=0, tiled=True)  9.48 us
    ppermute x7, starting transfers between devices, given(): return unpacked(lax.ppermute(partial, CORE, SWAP))  8.83 us
    ppermute x6, starting transfers between devices, around(): return [lax.ppermute(block, axis, way) for way in WAYS]  8.54 us
    ppermute x3, starting transfers between devices, losses(): piece = pair if way is None else lax.ppermute(pair, RING, way)  5.74 us
  transfers between devices with their start and end apart: 30, of which 10 were waited for; matrix products, arithmetic and copies ran while one was open for 22% of the time, Pallas kernels for 3%

profile of v1, /device:TPU:1, one launch (start us, length us, event | category | flops | bytes accessed | tf_op | source)
XLA Modules:
  0.0 168.7 jit_solution(3983651487496248047)
XLA Ops:
  1.6 3.6 %collective-permute-start.1 = (bf16[2,4,8,896]{3,2,1,0:T(8,128)(2,1)S(1)}, bf16[2,4,8,896]{3,2,1,0:T(8,128)(2,1)S(1)}, u32[]{:S(2)}, u32[]{:S(2)}) collective-permute-start(bf16[2,4,8,896]{3,2,1,0:T(8,128)(2,1)S(1)} %get-tuple-element.52), channel_id=1, source_target_pairs={{0,24},{8,0},{16,8},{24,16},{1,25},{9,1},{17,9},{25,17},{2,26},{10... | collective-permute-start | bytes 344072 | tf_op jit(solution)/shard_map/ppermute | solution.py:104
  9.3 4.0 %collective-permute-done = bf16[2,4,8,896]{3,2,1,0:T(8,128)(2,1)S(1)} collective-permute-done((bf16[2,4,8,896]{3,2,1,0:T(8,128)(2,1)S(1)}, bf16[2,4,8,896]{3,2,1,0:T(8,128)(2,1)S(1)}, u32[]{:S(2)}, u32[]{:S(2)}) %collective-permute-start) | collective-permute-done | bytes 114720 | tf_op jit(solution)/shard_map/ppermute | solution.py:104
  13.4 2.6 %collective-permute-start.7 = (bf16[2,32,896]{2,1,0:T(8,128)(2,1)S(1)}, bf16[2,32,896]{2,1,0:T(8,128)(2,1)S(1)}, u32[]{:S(2)}, u32[]{:S(2)}) collective-permute-start(bf16[2,32,896]{2,1,0:T(8,128)(2,1)S(1)} %get-tuple-element.44), channel_id=1, source_target_pairs={{0,96},{32,64},{64,32},{96,0},{1,97},{33,65},{65,33},{97,1},{2,98}... | collective-permute-start | bytes 344072 | tf_op jit(solution)/shard_map/ppermute | solution.py:115
  16.0 5.2 %resident.1 = bf16[896,8192]{1,0:T(8,128)(2,1)S(1)} custom-call(bf16[896,8192]{1,0:T(8,128)(2,1)} %given.1), custom_call_target="tpu_custom_call" | custom-call | tf_op jit(solution)/shard_map/resident/pallas_call | solution.py:61
  22.0 2.4 %collective-permute-start.9 = (bf16[2,32,896]{2,1,0:T(8,128)(2,1)S(1)}, bf16[2,32,896]{2,1,0:T(8,128)(2,1)S(1)}, u32[]{:S(2)}, u32[]{:S(2)}) collective-permute-start(bf16[2,32,896]{2,1,0:T(8,128)(2,1)S(1)} %get-tuple-element.43), channel_id=1, source_target_pairs={{0,96},{32,0},{64,32},{96,64},{1,97},{33,1},{65,33},{97,65},{2,98}... | collective-permute-start | bytes 344072 | tf_op jit(solution)/shard_map/ppermute | solution.py:104
  24.5 5.5 %collective-permute-done.5 = bf16[2,32,896]{2,1,0:T(8,128)(2,1)S(1)} collective-permute-done((bf16[2,32,896]{2,1,0:T(8,128)(2,1)S(1)}, bf16[2,32,896]{2,1,0:T(8,128)(2,1)S(1)}, u32[]{:S(2)}, u32[]{:S(2)}) %collective-permute-start.5) | collective-permute-done | bytes 114720 | tf_op jit(solution)/shard_map/ppermute | solution.py:114
  30.0 2.3 %collective-permute-start.6 = (bf16[2,64,896]{2,1,0:T(8,128)(2,1)S(1)}, bf16[2,64,896]{2,1,0:T(8,128)(2,1)S(1)}, u32[]{:S(2)}, u32[]{:S(2)}) collective-permute-start(bf16[2,64,896]{2,1,0:T(8,128)(2,1)S(1)} %pad_maximum_fusion.5), channel_id=1, source_target_pairs={{0,96},{32,64},{64,32},{96,0},{1,97},{33,65},{65,33},{97,1},{2,98}... | collective-permute-start | bytes 688136 | tf_op jit(solution)/shard_map/ppermute | solution.py:116
  33.7 2.7 %collective-permute-start.13 = (f16[128,3968]{1,0:T(8,128)(2,1)S(1)}, f16[128,3968]{1,0:T(8,128)(2,1)S(1)}, u32[]{:S(2)}, u32[]{:S(2)}) collective-permute-start(f16[128,3968]{1,0:T(8,128)(2,1)S(1)} %fusion.4), channel_id=1, source_target_pairs={{0,1},{1,0},{2,3},{3,2},{4,5},{5,4},{6,7},{7,6},{8,9},{9,8},{10,11... | collective-permute-start | bytes 3047432 | tf_op jit(solution)/shard_map/ppermute | solution.py:124
  38.7 2.3 %multiply_convert_fusion.5 = f16[128,3968]{1,0:T(8,128)(2,1)} fusion(f16[128,3968]{1,0:T(8,128)(2,1)S(1)} %collective-permute-done.13, bf16[896,8192]{1,0:T(8,128)(2,1)S(1)} %resident.1, bf16[2,128,896]{2,1,0:T(8,128)(2,1)S(1)} %pad_maximum_fusion.3), kind=kOutput, calls=%fused_computation.48 | convolution fusion | flops 912703488 | bytes 9371648 | tf_op jit(solution)/shard_map/dot_general | solution.py:34
  42.5 2.3 %fusion.5 = f16[128,3968]{1,0:T(8,128)(2,1)} fusion(bf16[896,8192]{1,0:T(8,128)(2,1)S(1)} %resident.1, bf16[2,128,896]{2,1,0:T(8,128)(2,1)S(1)} %pad_maximum_fusion.1), kind=kOutput, calls=%fused_computation.12 | convolution fusion | flops 911179776 | bytes 8355840 | tf_op jit(solution)/shard_map/dot_general | solution.py:34
  46.1 2.3 %fusion.2 = f16[128,4224]{1,0:T(8,128)(2,1)} fusion(bf16[896,8192]{1,0:T(8,128)(2,1)S(1)} %resident.1, bf16[2,128,896]{2,1,0:T(8,128)(2,1)S(1)} %pad_maximum_fusion.2), kind=kOutput, calls=%fused_computation.6 | convolution fusion | flops 969965568 | bytes 8880128 | tf_op jit(solution)/shard_map/dot_general | solution.py:34
  50.2 3.3 %collective-permute-start.28 = (s32[2,64]{1,0:T(2,128)S(1)}, s32[2,64]{1,0:T(2,128)S(1)}, u32[]{:S(2)}, u32[]{:S(2)}) collective-permute-start(s32[2,64]{1,0:T(2,128)S(1)} %pad_add_fusion), channel_id=1, source_target_pairs={{0,4},{2,6},{4,0},{6,2},{1,5},{3,7},{5,1},{7,3},{8,12},{10,14},{12... | collective-permute-start | bytes 1544 | tf_op jit(solution)/shard_map/ppermute | solution.py:95
  54.4 3.5 %collective-permute-done.3 = bf16[2,32,896]{2,1,0:T(8,128)(2,1)S(1)} collective-permute-done((bf16[2,32,896]{2,1,0:T(8,128)(2,1)S(1)}, bf16[2,32,896]{2,1,0:T(8,128)(2,1)S(1)}, u32[]{:S(2)}, u32[]{:S(2)}) %collective-permute-start.3) | collective-permute-done | bytes 114720 | tf_op jit(solution)/shard_map/ppermute | solution.py:119
  57.9 2.1 %collective-permute-start.4 = (bf16[2,64,896]{2,1,0:T(8,128)(2,1)S(1)}, bf16[2,64,896]{2,1,0:T(8,128)(2,1)S(1)}, u32[]{:S(2)}, u32[]{:S(2)}) collective-permute-start(bf16[2,64,896]{2,1,0:T(8,128)(2,1)S(1)} %pad_maximum_fusion.4), channel_id=1, source_target_pairs={{0,96},{32,64},{64,32},{96,0},{1,97},{33,65},{65,33},{97,1},{2,98}... | collective-permute-start | bytes 688136 | tf_op jit(solution)/shard_map/ppermute | solution.py:120
  60.1 5.7 %multiply_convert_fusion.4 = f16[128,3968]{1,0:T(8,128)(2,1)} fusion(f16[128,3968]{1,0:T(8,128)(2,1)} %collective-permute-done.14, bf16[896,8192]{1,0:T(8,128)(2,1)} %copy-done, bf16[2,128,896]{2,1,0:T(8,128)(2,1)S(1)} %pad_maximum_fusion.1), kind=kOutput, calls=%fused_computation.47 | convolution fusion | flops 912703488 | bytes 9371648 | tf_op jit(solution)/shard_map/dot_general | solution.py:34
  65.8 6.5 %multiply_convert_fusion.1 = f16[128,4224]{1,0:T(8,128)(2,1)} fusion(f16[128,4224]{1,0:T(8,128)(2,1)} %collective-permute-done.15, bf16[896,8192]{1,0:T(8,128)(2,1)} %copy-done, bf16[2,128,896]{2,1,0:T(8,128)(2,1)S(1)} %pad_maximum_fusion.2), kind=kOutput, calls=%fused_computation.39 | convolution fusion | flops 971587584 | bytes 9961472 | tf_op jit(solution)/shard_map/dot_general | solution.py:34
  73.6 2.9 %collective-permute-start.17 = (f16[128,3968]{1,0:T(8,128)(2,1)S(1)}, f16[128,3968]{1,0:T(8,128)(2,1)S(1)}, u32[]{:S(2)}, u32[]{:S(2)}) collective-permute-start(f16[128,3968]{1,0:T(8,128)(2,1)S(1)} %fusion.6), channel_id=1, source_target_pairs={{0,1},{1,0},{2,3},{3,2},{4,5},{5,4},{6,7},{7,6},{8,9},{9,8},{10,11... | collective-permute-start | bytes 3047432 | tf_op jit(solution)/shard_map/ppermute | solution.py:124
  85.2 2.4 %fusion = f16[128,8192]{1,0:T(8,128)(2,1)S(1)} fusion(bf16[896,8192]{1,0:T(8,128)(2,1)S(1)} %copy-done.1, bf16[2,128,896]{2,1,0:T(8,128)(2,1)S(1)} %pad_maximum_fusion), kind=kOutput, calls=%fused_computation.1 | convolution fusion | flops 1881145344 | bytes 17006592 | tf_op jit(solution)/shard_map/dot_general | solution.py:34
  89.2 12.8 %collective-permute-done.23 = f16[128,3968]{1,0:T(8,128)(2,1)S(1)} collective-permute-done((f16[128,3968]{1,0:T(8,128)(2,1)}, f16[128,3968]{1,0:T(8,128)(2,1)S(1)}, u32[]{:S(2)}, u32[]{:S(2)}) %collective-permute-start.23) | collective-permute-done | bytes 1015840 | tf_op jit(solution)/shard_map/ppermute | solution.py:144
  105.7 2.4 %multiply_add_fusion = f32[128,8192]{1,0:T(8,128)S(1)} fusion(f16[128,8192]{1,0:T(8,128)(2,1)S(1)} %collective-permute-done.18, bf16[896,8192]{1,0:T(8,128)(2,1)S(1)} %copy-done.1, bf16[2,128,896]{2,1,0:T(8,128)(2,1)S(1)} %pad_maximum_fusion), kind=kOutput, calls=%fused_computation.14 | convolution fusion | flops 1882193920 | bytes 21200896 | tf_op jit(solution)/shard_map/dot_general | solution.py:34
  110.0 15.2 %collective-permute-done.19 = f16[128,4224]{1,0:T(8,128)(2,1)S(1)} collective-permute-done((f16[128,4224]{1,0:T(8,128)(2,1)}, f16[128,4224]{1,0:T(8,128)(2,1)S(1)}, u32[]{:S(2)}, u32[]{:S(2)}) %collective-permute-start.19) | collective-permute-done | bytes 1081376 | tf_op jit(solution)/shard_map/ppermute | solution.py:146
  127.0 22.9 %collective-permute-done.22 = f16[128,4224]{1,0:T(8,128)(2,1)S(1)} collective-permute-done((f16[128,4224]{1,0:T(8,128)(2,1)S(1)}, f16[128,4224]{1,0:T(8,128)(2,1)S(1)}, u32[]{:S(2)}, u32[]{:S(2)}) %collective-permute-start.22) | collective-permute-done | bytes 1081376 | tf_op jit(solution)/shard_map/ppermute | solution.py:148
  153.3 4.9 %all-to-all-start = ((f32[128,1,48]{2,1,0:T(1,128)}), f32[128,1,48]{2,1,0:T(1,128)S(1)}, u32[]{:S(2)}, u32[]{:S(2)}) async-start(f32[128,1,48]{2,1,0:T(1,128)} %bitcast.25), calls=%async_computation | async-start | bytes 131072 | tf_op jit(solution)/shard_map/all_to_all | solution.py:184
  158.2 9.5 %all-to-all-done = f32[128,1,48]{2,1,0:T(1,128)S(1)} async-done(((f32[128,1,48]{2,1,0:T(1,128)}), f32[128,1,48]{2,1,0:T(1,128)S(1)}, u32[]{:S(2)}, u32[]{:S(2)}) %all-to-all-start) | async-done | bytes 24608 | tf_op jit(solution)/shard_map/all_to_all | solution.py:184
  (110 shorter events, 38.3 us)
Async XLA Ops:
  1.6 7.7 %collective-permute-start.1 = (bf16[2,4,8,896]{3,2,1,0:T(8,128)(2,1)S(1)}, bf16[2,4,8,896]{3,2,1,0:T(8,128)(2,1)S(1)}, u32[]{:S(2)}, u32[]{:S(2)}) collective-permute-start(bf16[2,4,8,896]{3,2,1,0:T(8,128)(2,1)S(1)} %get-tuple-element.52), channel_id=1, source_target_pairs={{0,24},{8,0},{16,8},{24,16},{1,25},{9,1},{17,9},{25,17},{2,26},{10... | collective-permute-start | bytes 344072 | tf_op jit(solution)/shard_map/ppermute | solution.py:104
  5.3 8.0 %collective-permute-start = (bf16[2,4,8,896]{3,2,1,0:T(8,128)(2,1)S(1)}, bf16[2,4,8,896]{3,2,1,0:T(8,128)(2,1)S(1)}, u32[]{:S(2)}, u32[]{:S(2)}) collective-permute-start(bf16[2,4,8,896]{3,2,1,0:T(8,128)(2,1)S(1)} %get-tuple-element.52), channel_id=1, source_target_pairs={{0,8},{8,16},{16,24},{24,0},{1,9},{9,17},{17,25},{25,1},{2,10},{10... | collective-permute-start | bytes 344072 | tf_op jit(solution)/shard_map/ppermute | solution.py:104
  5.3 8.0 %collective-permute-start.2 = (bf16[2,4,8,896]{3,2,1,0:T(8,128)(2,1)S(1)}, bf16[2,4,8,896]{3,2,1,0:T(8,128)(2,1)S(1)}, u32[]{:S(2)}, u32[]{:S(2)}) collective-permute-start(bf16[2,4,8,896]{3,2,1,0:T(8,128)(2,1)S(1)} %get-tuple-element.52), channel_id=1, source_target_pairs={{0,16},{8,24},{16,0},{24,8},{1,17},{9,25},{17,1},{25,9},{2,18},{10... | collective-permute-start | bytes 344072 | tf_op jit(solution)/shard_map/ppermute | solution.py:104
  7.7 40.8 %collective-permute-start.25 = (s32[1,64]{1,0:T(1,128)S(1)}, s32[1,64]{1,0:T(1,128)S(1)}, u32[]{:S(2)}, u32[]{:S(2)}) collective-permute-start(s32[1,64]{1,0:T(1,128)S(1)} %get-tuple-element.62), channel_id=1, source_target_pairs={{0,1},{1,0},{2,3},{3,2},{4,5},{5,4},{6,7},{7,6},{8,9},{9,8},{10,11... | collective-permute-start | bytes 776 | tf_op jit(solution)/shard_map/ppermute | solution.py:92
  13.4 11.1 %collective-permute-start.7 = (bf16[2,32,896]{2,1,0:T(8,128)(2,1)S(1)}, bf16[2,32,896]{2,1,0:T(8,128)(2,1)S(1)}, u32[]{:S(2)}, u32[]{:S(2)}) collective-permute-start(bf16[2,32,896]{2,1,0:T(8,128)(2,1)S(1)} %get-tuple-element.44), channel_id=1, source_target_pairs={{0,96},{32,64},{64,32},{96,0},{1,97},{33,65},{65,33},{97,1},{2,98}... | collective-permute-start | bytes 344072 | tf_op jit(solution)/shard_map/ppermute | solution.py:115
  21.2 11.2 %collective-permute-start.11 = (bf16[2,32,896]{2,1,0:T(8,128)(2,1)S(1)}, bf16[2,32,896]{2,1,0:T(8,128)(2,1)S(1)}, u32[]{:S(2)}, u32[]{:S(2)}) collective-permute-start(bf16[2,32,896]{2,1,0:T(8,128)(2,1)S(1)} %get-tuple-element.43), channel_id=1, source_target_pairs={{0,64},{32,96},{64,0},{96,32},{1,65},{33,97},{65,1},{97,33},{2,66}... | collective-permute-start | bytes 344072 | tf_op jit(solution)/shard_map/ppermute | solution.py:104
  21.8 8.2 %collective-permute-start.10 = (bf16[2,32,896]{2,1,0:T(8,128)(2,1)S(1)}, bf16[2,32,896]{2,1,0:T(8,128)(2,1)S(1)}, u32[]{:S(2)}, u32[]{:S(2)}) collective-permute-start(bf16[2,32,896]{2,1,0:T(8,128)(2,1)S(1)} %get-tuple-element.43), channel_id=1, source_target_pairs={{0,32},{32,64},{64,96},{96,0},{1,33},{33,65},{65,97},{97,1},{2,34}... | collective-permute-start | bytes 344072 | tf_op jit(solution)/shard_map/ppermute | solution.py:104
  22.0 10.3 %collective-permute-start.9 = (bf16[2,32,896]{2,1,0:T(8,128)(2,1)S(1)}, bf16[2,32,896]{2,1,0:T(8,128)(2,1)S(1)}, u32[]{:S(2)}, u32[]{:S(2)}) collective-permute-start(bf16[2,32,896]{2,1,0:T(8,128)(2,1)S(1)} %get-tuple-element.43), channel_id=1, source_target_pairs={{0,96},{32,0},{64,32},{96,64},{1,97},{33,1},{65,33},{97,65},{2,98}... | collective-permute-start | bytes 344072 | tf_op jit(solution)/shard_map/ppermute | solution.py:104
  30.0 7.9 %collective-permute-start.8 = (bf16[2,64,896]{2,1,0:T(8,128)(2,1)S(1)}, bf16[2,64,896]{2,1,0:T(8,128)(2,1)S(1)}, u32[]{:S(2)}, u32[]{:S(2)}) collective-permute-start(bf16[2,64,896]{2,1,0:T(8,128)(2,1)S(1)} %pad_maximum_fusion.6), channel_id=1, source_target_pairs={{0,32},{32,0},{64,96},{96,64},{1,33},{33,1},{65,97},{97,65},{2,34}... | collective-permute-start | bytes 688136 | tf_op jit(solution)/shard_map/ppermute | solution.py:117
  30.0 7.8 %collective-permute-start.6 = (bf16[2,64,896]{2,1,0:T(8,128)(2,1)S(1)}, bf16[2,64,896]{2,1,0:T(8,128)(2,1)S(1)}, u32[]{:S(2)}, u32[]{:S(2)}) collective-permute-start(bf16[2,64,896]{2,1,0:T(8,128)(2,1)S(1)} %pad_maximum_fusion.5), channel_id=1, source_target_pairs={{0,96},{32,64},{64,32},{96,0},{1,97},{33,65},{65,33},{97,1},{2,98}... | collective-permute-start | bytes 688136 | tf_op jit(solution)/shard_map/ppermute | solution.py:116
  44.8 15.3 %collective-permute-start.14 = (f16[128,3968]{1,0:T(8,128)(2,1)}, f16[128,3968]{1,0:T(8,128)(2,1)}, u32[]{:S(2)}, u32[]{:S(2)}) collective-permute-start(f16[128,3968]{1,0:T(8,128)(2,1)} %fusion.5), channel_id=1, source_target_pairs={{0,1},{1,0},{2,3},{3,2},{4,5},{5,4},{6,7},{7,6},{8,9},{9,8},{10,11... | collective-permute-start | bytes 3047432 | tf_op jit(solution)/shard_map/ppermute | solution.py:124
  48.5 17.3 %collective-permute-start.15 = (f16[128,4224]{1,0:T(8,128)(2,1)}, f16[128,4224]{1,0:T(8,128)(2,1)}, u32[]{:S(2)}, u32[]{:S(2)}) collective-permute-start(f16[128,4224]{1,0:T(8,128)(2,1)} %fusion.2), channel_id=1, source_target_pairs={{0,1},{1,0},{2,3},{3,2},{4,5},{5,4},{6,7},{7,6},{8,9},{9,8},{10,11... | collective-permute-start | bytes 3244040 | tf_op jit(solution)/shard_map/ppermute | solution.py:124
  50.2 27.8 %collective-permute-start.28 = (s32[2,64]{1,0:T(2,128)S(1)}, s32[2,64]{1,0:T(2,128)S(1)}, u32[]{:S(2)}, u32[]{:S(2)}) collective-permute-start(s32[2,64]{1,0:T(2,128)S(1)} %pad_add_fusion), channel_id=1, source_target_pairs={{0,4},{2,6},{4,0},{6,2},{1,5},{3,7},{5,1},{7,3},{8,12},{10,14},{12... | collective-permute-start | bytes 1544 | tf_op jit(solution)/shard_map/ppermute | solution.py:95
  53.5 24.5 %collective-permute-start.27 = (s32[2,64]{1,0:T(2,128)S(1)}, s32[2,64]{1,0:T(2,128)S(1)}, u32[]{:S(2)}, u32[]{:S(2)}) collective-permute-start(s32[2,64]{1,0:T(2,128)S(1)} %pad_add_fusion), channel_id=1, source_target_pairs={{0,6},{2,0},{4,2},{6,4},{1,7},{3,1},{5,3},{7,5},{8,14},{10,8},{12,... | collective-permute-start | bytes 1544 | tf_op jit(solution)/shard_map/ppermute | solution.py:95
  57.9 20.2 %collective-permute-start.4 = (bf16[2,64,896]{2,1,0:T(8,128)(2,1)S(1)}, bf16[2,64,896]{2,1,0:T(8,128)(2,1)S(1)}, u32[]{:S(2)}, u32[]{:S(2)}) collective-permute-start(bf16[2,64,896]{2,1,0:T(8,128)(2,1)S(1)} %pad_maximum_fusion.4), channel_id=1, source_target_pairs={{0,96},{32,64},{64,32},{96,0},{1,97},{33,65},{65,33},{97,1},{2,98}... | collective-permute-start | bytes 688136 | tf_op jit(solution)/shard_map/ppermute | solution.py:120
  73.6 6.9 %collective-permute-start.17 = (f16[128,3968]{1,0:T(8,128)(2,1)S(1)}, f16[128,3968]{1,0:T(8,128)(2,1)S(1)}, u32[]{:S(2)}, u32[]{:S(2)}) collective-permute-start(f16[128,3968]{1,0:T(8,128)(2,1)S(1)} %fusion.6), channel_id=1, source_target_pairs={{0,1},{1,0},{2,3},{3,2},{4,5},{5,4},{6,7},{7,6},{8,9},{9,8},{10,11... | collective-permute-start | bytes 3047432 | tf_op jit(solution)/shard_map/ppermute | solution.py:124
  78.2 23.8 %collective-permute-start.23 = (f16[128,3968]{1,0:T(8,128)(2,1)}, f16[128,3968]{1,0:T(8,128)(2,1)S(1)}, u32[]{:S(2)}, u32[]{:S(2)}) collective-permute-start(f16[128,3968]{1,0:T(8,128)(2,1)} %multiply_convert_fusion.5), channel_id=1, source_target_pairs={{0,6},{2,0},{4,2},{6,4},{1,7},{3,1},{5,3},{7,5},{8,14},{10,8},{12,... | collective-permute-start | bytes 3047432 | tf_op jit(solution)/shard_map/ppermute | solution.py:144
  79.1 25.9 %collective-permute-start.21 = (f16[128,4224]{1,0:T(8,128)(2,1)S(1)}, f16[128,4224]{1,0:T(8,128)(2,1)S(1)}, u32[]{:S(2)}, u32[]{:S(2)}) collective-permute-start(f16[128,4224]{1,0:T(8,128)(2,1)S(1)} %multiply_convert_fusion.2), channel_id=1, source_target_pairs={{0,2},{2,4},{4,6},{6,0},{1,3},{3,5},{5,7},{7,1},{8,10},{10,12},{12... | collective-permute-start | bytes 3244040 | tf_op jit(solution)/shard_map/ppermute | solution.py:143
  79.7 47.0 %collective-permute-start.20 = (f16[128,3968]{1,0:T(8,128)(2,1)}, f16[128,3968]{1,0:T(8,128)(2,1)S(1)}, u32[]{:S(2)}, u32[]{:S(2)}) collective-permute-start(f16[128,3968]{1,0:T(8,128)(2,1)} %multiply_convert_fusion.4), channel_id=1, source_target_pairs={{0,2},{2,4},{4,6},{6,0},{1,3},{3,5},{5,7},{7,1},{8,10},{10,12},{12... | collective-permute-start | bytes 3047432 | tf_op jit(solution)/shard_map/ppermute | solution.py:145
  80.5 44.7 %collective-permute-start.19 = (f16[128,4224]{1,0:T(8,128)(2,1)}, f16[128,4224]{1,0:T(8,128)(2,1)S(1)}, u32[]{:S(2)}, u32[]{:S(2)}) collective-permute-start(f16[128,4224]{1,0:T(8,128)(2,1)} %multiply_convert_fusion.1), channel_id=1, source_target_pairs={{0,6},{2,0},{4,2},{6,4},{1,7},{3,1},{5,3},{7,5},{8,14},{10,8},{12,... | collective-permute-start | bytes 3244040 | tf_op jit(solution)/shard_map/ppermute | solution.py:146
  87.6 18.1 %collective-permute-start.18 = (f16[128,8192]{1,0:T(8,128)(2,1)S(1)}, f16[128,8192]{1,0:T(8,128)(2,1)S(1)}, u32[]{:S(2)}, u32[]{:S(2)}) collective-permute-start(f16[128,8192]{1,0:T(8,128)(2,1)S(1)} %fusion), channel_id=1, source_target_pairs={{0,1},{1,0},{2,3},{3,2},{4,5},{5,4},{6,7},{7,6},{8,9},{9,8},{10,11... | collective-permute-start | bytes 6291464 | tf_op jit(solution)/shard_map/ppermute | solution.py:124
  102.4 47.9 %collective-permute-start.24 = (f16[128,3968]{1,0:T(8,128)(2,1)S(1)}, f16[128,3968]{1,0:T(8,128)(2,1)S(1)}, u32[]{:S(2)}, u32[]{:S(2)}) collective-permute-start(f16[128,3968]{1,0:T(8,128)(2,1)S(1)} %multiply_convert_fusion.3), channel_id=1, source_target_pairs={{0,6},{2,0},{4,2},{6,4},{1,7},{3,1},{5,3},{7,5},{8,14},{10,8},{12,... | collective-permute-start | bytes 3047432 | tf_op jit(solution)/shard_map/ppermute | solution.py:149
  105.3 44.5 %collective-permute-start.22 = (f16[128,4224]{1,0:T(8,128)(2,1)S(1)}, f16[128,4224]{1,0:T(8,128)(2,1)S(1)}, u32[]{:S(2)}, u32[]{:S(2)}) collective-permute-start(f16[128,4224]{1,0:T(8,128)(2,1)S(1)} %multiply_convert_fusion), channel_id=1, source_target_pairs={{0,2},{2,4},{4,6},{6,0},{1,3},{3,5},{5,7},{7,1},{8,10},{10,12},{12... | collective-permute-start | bytes 3244040 | tf_op jit(solution)/shard_map/ppermute | solution.py:148
  153.3 14.4 %all-to-all-start = ((f32[128,1,48]{2,1,0:T(1,128)}), f32[128,1,48]{2,1,0:T(1,128)S(1)}, u32[]{:S(2)}, u32[]{:S(2)}) async-start(f32[128,1,48]{2,1,0:T(1,128)} %bitcast.25), calls=%async_computation | async-start | bytes 131072 | tf_op jit(solution)/shard_map/all_to_all | solution.py:184
  (10 other events, 69.7 us)
